TPU v7x, 32 devices: a whole 2x2x4 slice. The times are simulated.
32 devices in a mesh: dom: 4 (over x, core), grp: 8 (over z, y).
Axes of the slice: x: 2, y: 2, z: 4, core: 2. Of those that a mesh axis runs over, the one named last changes fastest.
Arguments:
- features: bfloat16 [131072, 256], P(('dom', 'grp')), may hold values from -6 to 6
- w_fine: bfloat16 [256, 256], replicated, may hold values from -0.375 to 0.375
- adj_tiles: bfloat16 [1024, 20, 128, 128], P(('dom', 'grp')), may hold values from -0.125 to 0.125
- tile_cols: int32 [1024, 20], P(('dom', 'grp')), may hold values from 0 to 39
- tile_count: int32 [1024], P(('dom', 'grp')), may hold values from 1 to 20, as said below
- send_lower: int32 [128], P(('dom', 'grp')), may hold values from 0 to 31
- send_upper: int32 [128], P(('dom', 'grp')), may hold values from 0 to 31
- assign: int32 [131072], P(('dom', 'grp')), may hold values from 0 to 1023, as said below
- w_coarse: bfloat16 [256, 256], replicated, may hold values from -0.375 to 0.375
- coarse_adj: bfloat16 [1024, 1024], P(('dom', 'grp')), may hold values from -0.1875 to 0.1875
Outputs:
- output: bfloat16 [131072, 256], P(('dom', 'grp'))
Inputs may be any that keep to these rules, and one draw needn't show every extreme that they name: The first tile_count[r] slots of block row r are live; the others are ignored. `assign`: every coarse node is the coarse node of at least one vertex.
All inputs are finite; a program needn't handle non-finite values.
Results may differ from a plain program's by a relative error of at most 0.011.
Values may be sent and summed in bfloat16 or wider, within the bound.
No kernel may reach another device: no remote copies, remote signals or barrier semaphores. Data moves between devices by JAX's collectives and lax.ppermute only.
A program may use at most 192 MiB of HBM per device.

v0:
```python
import jax
import jax.numpy as jnp
from jax import lax
from jax.sharding import PartitionSpec as P

NC = 1024


def with_halo(shard, sides, width):
    for axis, dim in sides:
        peers, length = (lax.axis_size(axis), shard.shape[dim])
        up = [(i, (i + 1) % peers) for i in range(peers)]
        down = [(j, i) for i, j in up]
        last = lax.slice_in_dim(shard, length - width, length, axis=dim)
        initial = lax.slice_in_dim(shard, 0, width, axis=dim)
        before = lax.ppermute(last, axis, up)
        after = lax.ppermute(initial, axis, down)
        shard = jnp.concatenate([before, shard, after], axis=dim)
    return shard


def finish(coarse_sums, counts, w_coarse):
    coarse = (coarse_sums / jnp.sqrt(counts)[:, None]).astype(jnp.bfloat16)
    return jnp.dot(coarse, w_coarse, preferred_element_type=jnp.float32).astype(jnp.bfloat16)


def per_device(
    features,
    w_fine,
    adj_tiles,
    tile_cols,
    tile_count,
    send_lower,
    send_upper,
    assign,
    w_coarse,
    coarse_adj,
):
    vertex_rows = features.shape[0]
    feat_width = features.shape[1]
    block_rows = adj_tiles.shape[2]
    slot_count = adj_tiles.shape[1]
    block_count = vertex_rows // block_rows
    halo_blocks = send_lower.shape[0]
    projected = jnp.dot(features, w_fine, preferred_element_type=jnp.float32).astype(jnp.bfloat16)
    own_blocks = projected.reshape(block_count, block_rows, feat_width)
    lower_sel = own_blocks[send_lower]
    upper_sel = own_blocks[send_upper]
    packed = jnp.concatenate([lower_sel, upper_sel], axis=0).reshape(
        2 * halo_blocks * block_rows, feat_width
    )
    padded = with_halo(packed, (("dom", 0),), halo_blocks * block_rows)
    from_below = padded[: halo_blocks * block_rows].reshape(halo_blocks, block_rows, feat_width)
    from_above = padded[-halo_blocks * block_rows :].reshape(halo_blocks, block_rows, feat_width)
    extended = jnp.concatenate([own_blocks, from_below, from_above], axis=0)
    coarse_sums = jax.ops.segment_sum(features.astype(jnp.float32), assign, num_segments=NC)
    counts = jax.ops.segment_sum(jnp.ones((vertex_rows,), jnp.float32), assign, num_segments=NC)
    live_mask = jnp.arange(slot_count)[None, :] < tile_count[:, None]
    kept = jnp.where(live_mask[:, :, None, None], adj_tiles, jnp.zeros((), jnp.bfloat16))
    picked = extended[tile_cols]
    fine_out = jnp.einsum("rkij,rkjf->rif", kept, picked, preferred_element_type=jnp.float32)
    fine_out = fine_out.reshape(vertex_rows, feat_width)
    total_sums, total_counts = lax.psum((coarse_sums, counts), ("dom", "grp"))
    coarse_all = finish(total_sums, total_counts, w_coarse)
    own_count = coarse_adj.shape[0]
    own_start = (lax.axis_index("dom") * lax.axis_size("grp") + lax.axis_index("grp")) * own_count
    self_rows = lax.dynamic_slice_in_dim(coarse_all, own_start, own_count, 0)
    coarse_mixed = (
        self_rows.astype(jnp.float32)
        + jnp.dot(coarse_adj, coarse_all, preferred_element_type=jnp.float32)
    ).astype(jnp.bfloat16)
    coarse_every = lax.all_gather(coarse_mixed, ("dom", "grp"), axis=0, tiled=True)
    return jax.nn.relu(fine_out + coarse_every[assign].astype(jnp.float32)).astype(jnp.bfloat16)


def solution(mesh):
    return jax.shard_map(
        per_device,
        mesh=mesh,
        in_specs=(
            P(("dom", "grp"), None),
            P(),
            P(("dom", "grp"), None, None, None),
            P(("dom", "grp"), None),
            P(("dom", "grp")),
            P(("dom", "grp")),
            P(("dom", "grp")),
            P(("dom", "grp")),
            P(),
            P(("dom", "grp"), None),
        ),
        out_specs=P(("dom", "grp"), None),
        check_vma=False,
    )
```

profile of v0, /device:TPU:0, one launch (start us, length us, event | category | flops | bytes accessed | tf_op | source)
XLA Modules:
  0.0 263.3 jit_solution(4760606489332169957)
XLA Ops:
  6.5 0.0 copy-start
  6.5 0.0 copy-start.8
  6.5 0.0 copy-start.4
  6.5 0.0 all-reduce.2.cloned.1.call-start
  6.5 0.7 compare_select_fusion.2
  7.2 0.2 copy-done
  7.5 2.3 convolution_convert_fusion
  9.8 0.0 copy-start.2
  9.8 0.0 copy-start.5
  9.8 0.0 copy-start.6
  9.8 0.6 gather_fusion.1
  10.4 2.4 collective-permute-start.1
  12.8 0.0 copy-done.8
  12.8 0.6 gather_fusion
  13.4 0.1 collective-permute-start
  13.5 0.0 copy-done.4
  13.5 21.9 %scatter_custom_fusion = f32[1024,256]{1,0:T(8,128)} fusion(s32[4096]{0:T(1024)S(1)} %copy-done.4, bf16[4096,256]{1,0:T(8,128)(2,1)} %param.10, f32[]{:T(128)} %constant.14.clone.1), kind=kCustom, calls=%fused_computation.14 | custom fusion | flops 2097152 | bytes 3145732 | tf_op jit(solution)/shard_map/scatter-add | solution.py:56
  35.4 0.0 all-reduce.2.cloned.1.call-update
  35.4 0.0 copy-done.5
  35.4 0.1 copy.11
  35.5 0.1 reshape.59
  35.6 0.0 copy-done.6
  35.6 0.1 iota_compare_fusion
  35.7 28.8 %scatter_custom_fusion.1 = f32[1024]{0:T(1024)S(1)} fusion(s32[4096]{0:T(1024)S(1)} %copy-done.4, f32[4096]{0:T(1024)S(1)} %broadcast.23, f32[]{:T(128)} %constant.14.clone.1), kind=kCustom, calls=%fused_computation.32 | custom fusion | flops 4096 | bytes 4100 | tf_op jit(solution)/shard_map/scatter-add | solution.py:57
  64.5 40.2 %psum.15 = f32[1024]{0:T(1024)S(1)} all-reduce(f32[1024]{0:T(1024)S(1)} %scatter_custom_fusion.1), channel_id=1, replica_groups=mesh['dom'=4,'grp'=8] {'dom','grp'}, use_global_device_ids=true, to_apply=%region_3.4 | all-reduce | flops 1024 | bytes 8192 | tf_op jit(solution)/shard_map/psum | solution.py:63
  104.7 0.0 collective-permute-done.1
  104.7 0.0 collective-permute-done
  104.7 0.0 copy-done.2
  104.8 1.9 pad_maximum_fusion
  106.7 19.3 %gather_fusion.2 = bf16[640,128,256]{2,1,0:T(8,128)(2,1)} fusion(bf16[40,128,256]{2,1,0:T(8,128)(2,1)S(1)} %pad_maximum_fusion, s32[1024]{0:T(1024)S(1)} %pad_clamp_fusion), kind=kCustom, calls=%fused_computation.2 | custom fusion | bytes 83888640 | tf_op jit(solution)/shard_map/gather | solution.py:60
  126.0 0.0 copy-start.7
  126.0 0.0 copy-start.3
  126.0 23.5 %fusion = f32[32,128,256,1]{2,1,3,0:T(8,128)} fusion(bf16[32,20,128,256]{3,2,1,0:T(8,128)(2,1)} %bitcast.27, bf16[32,20,128,128]{3,2,1,0:T(8,128)(2,1)} %param.12, pred[32,20]{1,0:T(8,128)(4,1)S(1)} %iota_compare_fusion), kind=kOutput, calls=%fused_computation.6 | convolution fusion | flops 5379194880 | bytes 67109504 | tf_op jit(solution)/shard_map/rkij,rkjf->rif/dot_general | solution.py:61
  149.4 18.4 %all-reduce.2.cloned.1.call-done = f32[1024,256]{1,0:T(8,128)} async-done(((f32[1024,256]{1,0:T(8,128)}), f32[1024,256]{1,0:T(8,128)}) %all-reduce.2.cloned.1.call-update) | async-done | bytes 1048592 | tf_op jit(solution)/shard_map/psum | solution.py:63
  167.8 0.0 copy-done.7
  167.8 1.6 convolution_convert_fusion.1
  169.4 0.0 copy-done.3
  169.4 0.2 fusion.9
  169.6 68.2 %all_gather.3 = bf16[1024,256]{1,0:T(8,128)(2,1)S(1)} all-gather(bf16[32,256]{1,0:T(8,128)(2,1)S(1)} %fusion.9), channel_id=1, replica_groups=mesh['dom'=4,'grp'=8] {'dom','grp'}, dimensions={0}, use_global_device_ids=true | all-gather | bytes 540672 | tf_op jit(solution)/shard_map/all_gather | solution.py:72
  237.8 0.0 copy-start.1
  237.8 14.6 %gather_fusion.3 = bf16[4096,256]{1,0:T(8,128)(2,1)S(1)} fusion(bf16[1024,256]{1,0:T(8,128)(2,1)S(1)} %all_gather.3, s32[4096]{0:T(1024)S(1)} %fusion.11), kind=kCustom, calls=%fused_computation.3 | custom fusion | bytes 4210688 | tf_op jit(solution)/shard_map/gather | solution.py:73
  252.5 4.0 %fusion.5 = bf16[4096,256]{1,0:T(8,128)(2,1)} fusion(f32[32,128,256,1]{2,1,3,0:T(8,128)} %fusion, bf16[4096,256]{1,0:T(8,128)(2,1)S(1)} %gather_fusion.3), kind=kLoop, calls=%fused_computation.13 | loop fusion | flops 4194304 | bytes 8388608 | tf_op jit(solution)/shard_map/convert_element_type | solution.py:73
  256.5 0.0 copy-done.1
  (8 shorter events, 0.0 us)
Async XLA Ops:
  6.5 0.9 copy-start
  6.5 6.3 %copy-start.8 = (s32[4]{0:T(128)S(1)}, s32[4]{0:T(128)}, u32[]{:S(2)}) copy-start(s32[4]{0:T(128)} %param.16) | copy-start | bytes 52
  6.5 6.9 %copy-start.4 = (s32[4096]{0:T(1024)S(1)}, s32[4096]{0:T(1024)}, u32[]{:S(2)}) copy-start(s32[4096]{0:T(1024)} %param.17) | copy-start | bytes 49156
  6.5 161.3 %all-reduce.2.cloned.1.call-start = ((), (), s32[]{:S(2)}) async-start(), calls=%async_computation | async-start | bytes 2097152 | tf_op jit(solution)/shard_map/psum | solution.py:63
  9.8 95.0 %copy-start.2 = (bf16[4096,256]{1,0:T(8,128)(2,1)}, bf16[4096,256]{1,0:T(8,128)(2,1)S(1)}, u32[]{:S(2)}) copy-start(bf16[4096,256]{1,0:T(8,128)(2,1)S(1)} %convolution_convert_fusion) | copy-start | bytes 6291460
  9.8 25.6 %copy-start.5 = (s32[32,20]{0,1:T(8,128)S(1)}, s32[32,20]{0,1:T(8,128)}, u32[]{:S(2)}) copy-start(s32[32,20]{0,1:T(8,128)} %param.13) | copy-start | bytes 7684
  9.8 25.8 %copy-start.6 = (s32[32]{0:T(128)S(1)}, s32[32]{0:T(128)}, u32[]{:S(2)}) copy-start(s32[32]{0:T(128)} %param.14) | copy-start | bytes 388
  10.4 94.4 %collective-permute-start.1 = (bf16[512,256]{1,0:T(8,128)(2,1)S(1)}, bf16[512,256]{1,0:T(8,128)(2,1)S(1)}, u32[]{:S(2)}, u32[]{:S(2)}) collective-permute-start(bf16[512,256]{1,0:T(8,128)(2,1)S(1)} %bitcast.33), channel_id=1, source_target_pairs={{8,0},{16,8},{24,16},{0,24},{9,1},{17,9},{25,17},{1,25},{10,2},{18... | collective-permute-start | bytes 786440 | tf_op jit(solution)/shard_map/ppermute | solution.py:17
  13.4 91.3 %collective-permute-start = (bf16[512,256]{1,0:T(8,128)(2,1)S(1)}, bf16[512,256]{1,0:T(8,128)(2,1)S(1)}, u32[]{:S(2)}, u32[]{:S(2)}) collective-permute-start(bf16[512,256]{1,0:T(8,128)(2,1)S(1)} %bitcast.34), channel_id=1, source_target_pairs={{0,8},{8,16},{16,24},{24,0},{1,9},{9,17},{17,25},{25,1},{2,10},{10... | collective-permute-start | bytes 786440 | tf_op jit(solution)/shard_map/ppermute | solution.py:16
  126.0 41.9 %copy-start.7 = (bf16[256,256]{1,0:T(8,128)(2,1)S(1)}, bf16[256,256]{1,0:T(8,128)(2,1)}, u32[]{:S(2)}) copy-start(bf16[256,256]{1,0:T(8,128)(2,1)} %param.18) | copy-start | bytes 393220
  126.0 43.5 %copy-start.3 = (bf16[32,1024]{1,0:T(8,128)(2,1)S(1)}, bf16[32,1024]{1,0:T(8,128)(2,1)}, u32[]{:S(2)}) copy-start(bf16[32,1024]{1,0:T(8,128)(2,1)} %param.19) | copy-start | bytes 196612
  237.8 18.7 %copy-start.1 = (bf16[256,256]{1,0:T(8,128)(2,1)S(1)}, bf16[256,256]{1,0:T(8,128)(2,1)}, u32[]{:S(2)}) copy-start(bf16[256,256]{1,0:T(8,128)(2,1)} %param.11) | copy-start | bytes 393220
Sparse Core Ops, SparseCore 0:
  35.5 132.2 all-reduce.1
where the time goes:
time: 264 us; the launch traced here: 263 us
  blocking collectives  108 us (41%)
  other arithmetic  57.5 us (22%)
  local copies, waits for them, and re-layouts  35.4 us (13%)
  matrix products  27.6 us (10%)
  waiting for transfers between devices  18.4 us (7%)
  between operations  13.6 us (5%)
    all_gather x1, blocking collectives, per_device(): lax.all_gather(coarse_mixed, ('dom', 'grp'), axis=0, tiled=True)  68.2 us
    psum x1, blocking collectives, per_device(): total_sums, total_counts = lax.psum((coarse_sums, counts), ('dom', 'grp'))  40.2 us
    scatter-add x1, other arithmetic, per_device(): jax.ops.segment_sum(jnp.ones((vertex_rows,), jnp.float32), assign, num_se...  28.8 us
    dot_general x1, matrix products, per_device(): jnp.einsum('rkij,rkjf->rif', kept, picked, preferred_element_type=jnp.flo...  23.5 us
    scatter-add x1, other arithmetic, per_device(): jax.ops.segment_sum(features.astype(jnp.float32), assign, num_segments=NC)  21.9 us
    gather x1, local copies, waits for them, and re-layouts, per_device(): picked = extended[tile_cols]  19.3 us
    psum x1, waiting for transfers between devices, per_device(): total_sums, total_counts = lax.psum((coarse_sums, counts), ('dom', 'grp'))  18.4 us
    gather x1, local copies, waits for them, and re-layouts, per_device(): coarse_every[assign].astype(jnp.float32)  14.6 us
  transfers between devices with their start and end apart: 3, of which 1 were waited for; matrix products, arithmetic and copies ran while one was open for 37% of the time, Pallas kernels for 0%

commit v1 on v0

--- a/solution.py
+++ b/solution.py
@@ -60,7 +60,7 @@
     picked = extended[tile_cols]
     fine_out = jnp.einsum("rkij,rkjf->rif", kept, picked, preferred_element_type=jnp.float32)
     fine_out = fine_out.reshape(vertex_rows, feat_width)
-    total_sums, total_counts = lax.psum((coarse_sums, counts), ("dom", "grp"))
+    total_sums, total_counts = lax.psum(lax.psum((coarse_sums, counts), "grp"), "dom")
     coarse_all = finish(total_sums, total_counts, w_coarse)
     own_count = coarse_adj.shape[0]
     own_start = (lax.axis_index("dom") * lax.axis_size("grp") + lax.axis_index("grp")) * own_count

time: 264 us -> 250 us (0.947)
  blocking collectives: 108 us -> 97.6 us
  waiting for transfers between devices: 18.4 us -> 15 us
    psum x1 -> x2, blocking collectives: 40.2 us -> 27.6 us  [the longest x1 21.8 us: per_device(): lax.psum((coarse_sums, counts), 'grp')]
    psum x1 -> x2, waiting for transfers between devices: 18.4 us -> 14.9 us  [the longest x1 14.5 us: per_device(): lax.psum(lax.psum((coarse_sums, counts), 'grp'), 'dom')]
  transfers between devices with their start and end apart: 3 -> 4, of which waited for: 1 -> 2; matrix products, arithmetic and copies ran while one was open for 37% -> 39% of each run, Pallas kernels for 0% -> 0%
where the time goes in v1:
time: 250 us; the launch traced here: 249 us
  blocking collectives  97.6 us (39%)
  other arithmetic  57.4 us (23%)
  local copies, waits for them, and re-layouts  35.4 us (14%)
  matrix products  27.9 us (11%)
  waiting for transfers between devices  15 us (6%)
  between operations  13.6 us (5%)
  starting transfers between devices  2.55 us (1%)
    all_gather x1, blocking collectives, per_device(): lax.all_gather(coarse_mixed, ('dom', 'grp'), axis=0, tiled=True)  70 us
    scatter-add x1, other arithmetic, per_device(): jax.ops.segment_sum(jnp.ones((vertex_rows,), jnp.float32), assign, num_se...  28.8 us
    dot_general x1, matrix products, per_device(): jnp.einsum('rkij,rkjf->rif', kept, picked, preferred_element_type=jnp.flo...  23.8 us
    scatter-add x1, other arithmetic, per_device(): jax.ops.segment_sum(features.astype(jnp.float32), assign, num_segments=NC)  21.9 us
    psum x1, blocking collectives, per_device(): lax.psum((coarse_sums, counts), 'grp')  21.8 us
    gather x1, local copies, waits for them, and re-layouts, per_device(): picked = extended[tile_cols]  19.3 us
    gather x1, local copies, waits for them, and re-layouts, per_device(): coarse_every[assign].astype(jnp.float32)  14.6 us
    psum x1, waiting for transfers between devices, per_device(): lax.psum(lax.psum((coarse_sums, counts), 'grp'), 'dom')  14.5 us
  transfers between devices with their start and end apart: 4, of which 2 were waited for; matrix products, arithmetic and copies ran while one was open for 39% of the time, Pallas kernels for 0%

profile of v1, /device:TPU:0, one launch (start us, length us, event | category | flops | bytes accessed | tf_op | source)
XLA Modules:
  0.0 249.4 jit_solution(9443433864067554659)
XLA Ops:
  6.5 0.0 copy-start
  6.5 0.0 copy-start.4
  6.5 0.0 all-reduce.3.cloned.1.call-start
  6.5 0.7 compare_select_fusion.2
  7.2 0.2 copy-done
  7.5 0.0 copy-start.8
  7.5 2.3 convolution_convert_fusion
  9.8 0.0 copy-start.2
  9.8 0.0 copy-start.5
  9.8 0.0 copy-start.6
  9.8 0.6 gather_fusion.1
  10.4 2.5 collective-permute-start.1
  12.8 0.0 copy-done.4
  12.8 21.9 %scatter_custom_fusion = f32[1024,256]{1,0:T(8,128)} fusion(s32[4096]{0:T(1024)S(1)} %copy-done.4, bf16[4096,256]{1,0:T(8,128)(2,1)} %param.10, f32[]{:T(128)} %constant.14.clone.1), kind=kCustom, calls=%fused_computation.14 | custom fusion | flops 2097152 | bytes 3145732 | tf_op jit(solution)/shard_map/scatter-add | solution.py:56
  34.7 0.0 all-reduce.3.cloned.1.call-update
  34.7 0.0 all-reduce.5.cloned.1.call-start
  34.8 0.0 copy-done.8
  34.8 0.6 gather_fusion
  35.4 0.1 collective-permute-start
  35.5 0.0 copy-done.5
  35.5 0.1 copy.11
  35.6 0.1 reshape.59
  35.7 0.0 copy-done.6
  35.7 0.1 iota_compare_fusion
  35.8 28.8 %scatter_custom_fusion.1 = f32[1024]{0:T(1024)S(1)} fusion(s32[4096]{0:T(1024)S(1)} %copy-done.4, f32[4096]{0:T(1024)S(1)} %broadcast.23, f32[]{:T(128)} %constant.14.clone.1), kind=kCustom, calls=%fused_computation.32 | custom fusion | flops 4096 | bytes 4100 | tf_op jit(solution)/shard_map/scatter-add | solution.py:57
  64.6 21.8 %psum.30 = f32[1024]{0:T(1024)S(1)} all-reduce(f32[1024]{0:T(1024)S(1)} %scatter_custom_fusion.1), channel_id=1, replica_groups=mesh['dom'=4,'grp'=8] {'grp'}, use_global_device_ids=true, to_apply=%region_4.5 | all-reduce | flops 1024 | bytes 8192 | tf_op jit(solution)/shard_map/psum | solution.py:63
  86.3 5.8 %psum.31 = f32[1024]{0:T(1024)S(1)} all-reduce(f32[1024]{0:T(1024)S(1)} %psum.30), channel_id=1, replica_groups=mesh['dom'=4,'grp'=8] {'dom'}, use_global_device_ids=true, to_apply=%region_5.6 | all-reduce | flops 1024 | bytes 8192 | tf_op jit(solution)/shard_map/psum | solution.py:63
  92.1 0.0 collective-permute-done.1
  92.2 0.0 collective-permute-done
  92.2 0.0 copy-done.2
  92.2 1.9 pad_maximum_fusion
  94.1 19.3 %gather_fusion.2 = bf16[640,128,256]{2,1,0:T(8,128)(2,1)} fusion(bf16[40,128,256]{2,1,0:T(8,128)(2,1)S(1)} %pad_maximum_fusion, s32[1024]{0:T(1024)S(1)} %pad_clamp_fusion), kind=kCustom, calls=%fused_computation.2 | custom fusion | bytes 83888640 | tf_op jit(solution)/shard_map/gather | solution.py:60
  113.4 0.5 all-reduce.3.cloned.1.call-done
  113.8 0.0 all-reduce.5.cloned.1.call-update
  113.8 0.0 copy-start.7
  113.8 0.0 copy-start.3
  113.9 23.8 %fusion = f32[32,128,256,1]{2,1,3,0:T(8,128)} fusion(bf16[32,20,128,256]{3,2,1,0:T(8,128)(2,1)} %bitcast.27, bf16[32,20,128,128]{3,2,1,0:T(8,128)(2,1)} %param.12, pred[32,20]{1,0:T(8,128)(4,1)S(1)} %iota_compare_fusion), kind=kOutput, calls=%fused_computation.6 | convolution fusion | flops 5379194880 | bytes 67109504 | tf_op jit(solution)/shard_map/rkij,rkjf->rif/dot_general | solution.py:61
  137.6 14.5 %all-reduce.5.cloned.1.call-done = f32[1024,256]{1,0:T(8,128)} async-done(((f32[1024,256]{1,0:T(8,128)}), f32[1024,256]{1,0:T(8,128)}) %all-reduce.5.cloned.1.call-update) | async-done | bytes 1048592 | tf_op jit(solution)/shard_map/psum | solution.py:63
  152.1 0.0 copy-done.7
  152.1 1.6 convolution_convert_fusion.1
  153.7 0.0 copy-done.3
  153.7 0.2 fusion.9
  153.9 70.0 %all_gather.3 = bf16[1024,256]{1,0:T(8,128)(2,1)S(1)} all-gather(bf16[32,256]{1,0:T(8,128)(2,1)S(1)} %fusion.9), channel_id=1, replica_groups=mesh['dom'=4,'grp'=8] {'dom','grp'}, dimensions={0}, use_global_device_ids=true | all-gather | bytes 540672 | tf_op jit(solution)/shard_map/all_gather | solution.py:72
  223.9 0.0 copy-start.1
  223.9 14.6 %gather_fusion.3 = bf16[4096,256]{1,0:T(8,128)(2,1)S(1)} fusion(bf16[1024,256]{1,0:T(8,128)(2,1)S(1)} %all_gather.3, s32[4096]{0:T(1024)S(1)} %fusion.11), kind=kCustom, calls=%fused_computation.3 | custom fusion | bytes 4210688 | tf_op jit(solution)/shard_map/gather | solution.py:73
  238.6 4.0 %fusion.5 = bf16[4096,256]{1,0:T(8,128)(2,1)} fusion(f32[32,128,256,1]{2,1,3,0:T(8,128)} %fusion, bf16[4096,256]{1,0:T(8,128)(2,1)S(1)} %gather_fusion.3), kind=kLoop, calls=%fused_computation.13 | loop fusion | flops 4194304 | bytes 8388608 | tf_op jit(solution)/shard_map/convert_element_type | solution.py:73
  242.6 0.0 copy-done.1
  (8 shorter events, 0.0 us)
Async XLA Ops:
  6.5 0.9 copy-start
  6.5 6.3 %copy-start.4 = (s32[4096]{0:T(1024)S(1)}, s32[4096]{0:T(1024)}, u32[]{:S(2)}) copy-start(s32[4096]{0:T(1024)} %param.17) | copy-start | bytes 49156
  6.5 107.3 %all-reduce.3.cloned.1.call-start = ((), (), s32[]{:S(2)}) async-start(), calls=%async_computation | async-start | bytes 2097152 | tf_op jit(solution)/shard_map/psum | solution.py:63
  7.5 27.3 %copy-start.8 = (s32[4]{0:T(128)S(1)}, s32[4]{0:T(128)}, u32[]{:S(2)}) copy-start(s32[4]{0:T(128)} %param.16) | copy-start | bytes 52
  9.8 82.4 %copy-start.2 = (bf16[4096,256]{1,0:T(8,128)(2,1)}, bf16[4096,256]{1,0:T(8,128)(2,1)S(1)}, u32[]{:S(2)}) copy-start(bf16[4096,256]{1,0:T(8,128)(2,1)S(1)} %convolution_convert_fusion) | copy-start | bytes 6291460
  9.8 25.7 %copy-start.5 = (s32[32,20]{0,1:T(8,128)S(1)}, s32[32,20]{0,1:T(8,128)}, u32[]{:S(2)}) copy-start(s32[32,20]{0,1:T(8,128)} %param.13) | copy-start | bytes 7684
  9.8 25.9 %copy-start.6 = (s32[32]{0:T(128)S(1)}, s32[32]{0:T(128)}, u32[]{:S(2)}) copy-start(s32[32]{0:T(128)} %param.14) | copy-start | bytes 388
  10.4 81.8 %collective-permute-start.1 = (bf16[512,256]{1,0:T(8,128)(2,1)S(1)}, bf16[512,256]{1,0:T(8,128)(2,1)S(1)}, u32[]{:S(2)}, u32[]{:S(2)}) collective-permute-start(bf16[512,256]{1,0:T(8,128)(2,1)S(1)} %bitcast.33), channel_id=1, source_target_pairs={{8,0},{16,8},{24,16},{0,24},{9,1},{17,9},{25,17},{1,25},{10,2},{18... | collective-permute-start | bytes 786440 | tf_op jit(solution)/shard_map/ppermute | solution.py:17
  34.7 117.4 %all-reduce.5.cloned.1.call-start = ((), (), s32[]{:S(2)}) async-start(), calls=%async_computation.1 | async-start | bytes 2097152 | tf_op jit(solution)/shard_map/psum | solution.py:63
  35.4 56.8 %collective-permute-start = (bf16[512,256]{1,0:T(8,128)(2,1)S(1)}, bf16[512,256]{1,0:T(8,128)(2,1)S(1)}, u32[]{:S(2)}, u32[]{:S(2)}) collective-permute-start(bf16[512,256]{1,0:T(8,128)(2,1)S(1)} %bitcast.34), channel_id=1, source_target_pairs={{0,8},{8,16},{16,24},{24,0},{1,9},{9,17},{17,25},{25,1},{2,10},{10... | collective-permute-start | bytes 786440 | tf_op jit(solution)/shard_map/ppermute | solution.py:16
  113.8 38.3 %copy-start.7 = (bf16[256,256]{1,0:T(8,128)(2,1)S(1)}, bf16[256,256]{1,0:T(8,128)(2,1)}, u32[]{:S(2)}) copy-start(bf16[256,256]{1,0:T(8,128)(2,1)} %param.18) | copy-start | bytes 393220
  113.8 39.8 %copy-start.3 = (bf16[32,1024]{1,0:T(8,128)(2,1)S(1)}, bf16[32,1024]{1,0:T(8,128)(2,1)}, u32[]{:S(2)}) copy-start(bf16[32,1024]{1,0:T(8,128)(2,1)} %param.19) | copy-start | bytes 196612
  223.9 18.7 %copy-start.1 = (bf16[256,256]{1,0:T(8,128)(2,1)S(1)}, bf16[256,256]{1,0:T(8,128)(2,1)}, u32[]{:S(2)}) copy-start(bf16[256,256]{1,0:T(8,128)(2,1)} %param.11) | copy-start | bytes 393220
Sparse Core Ops, SparseCore 0:
  34.9 78.8 all-reduce.2
  116.2 35.8 all-reduce.4
